TPU v7x, 32 devices: a whole 2x2x4 slice. The times are simulated.
32 devices in a mesh: row: 8 (over y, x, core), gz: 4 (over z).
Axes of the slice: x: 2, y: 2, z: 4, core: 2. Of those that a mesh axis runs over, the one named last changes fastest.
Arguments:
- velocity_x: bfloat16 [2, 8, 1024, 1024], P(None, None, 'row', 'gz'), may hold values from -6 to 6
- velocity_y: bfloat16 [2, 8, 1024, 1024], P(None, None, 'row', 'gz'), may hold values from -6 to 6
- velocity_z: bfloat16 [2, 8, 1024, 1024], P(None, None, 'row', 'gz'), may hold values from -6 to 6
- spacing: float32 [64], replicated, may hold values from 0.5 to 2
- level_index: int32 [1024], replicated, may hold values from 0 to 63
- plane_index: int32 [8], replicated, may hold values from 4 to 128
Outputs:
- pressure: float32 [2, 8, 1024, 1024], P(None, None, 'row', 'gz')
All inputs are finite; a program needn't handle non-finite values.
Results may differ from a plain program's by a relative error of at most 0.002.
The roundings to bfloat16 on the way count: a program that leaves them out, or rounds other values in their place, can miss the bound.
Values may be sent and summed in bfloat16 or wider, within the bound.
A program may use at most 64 MiB of HBM per device.

v0:
```python
import math

import jax
import jax.numpy as jnp
from jax import lax
from jax.sharding import PartitionSpec as P

RADIX = 8


full_turn = 2.0 * math.pi
wave_unit = 2.0 * math.pi / 2048.0
highest = lax.Precision.HIGHEST


def shifted_2(array, axis, by):
    length = lax.axis_size(axis)
    pairs = [(i, i + by) for i in range(length) if 0 <= i + by < length]
    return lax.ppermute(array, axis, pairs)


def band_coefficients(cell_width):
    length = cell_width.shape[0]
    index = jnp.arange(length, dtype=jnp.int32)
    previous = jnp.concatenate([cell_width[:1], cell_width[:-1]])
    following = jnp.concatenate([cell_width[1:], cell_width[-1:]])
    lower_band = jnp.where(index > 0, 1.0 / (0.5 * (previous + cell_width) * cell_width), 0.0)
    upper_band = jnp.where(
        index < length - 1, 1.0 / (0.5 * (cell_width + following) * cell_width), 0.0
    )
    return (lower_band, upper_band)


def shifted(values, offset, dim_index, fill_value):
    length = values.shape[dim_index]
    pad_shape = list(values.shape)
    pad_shape[dim_index] = abs(offset)
    filler = jnp.full(pad_shape, fill_value, values.dtype)
    if offset > 0:
        kept = lax.slice_in_dim(values, 0, length - offset, axis=dim_index)
        return jnp.concatenate([filler, kept], axis=dim_index)
    kept = lax.slice_in_dim(values, -offset, length, axis=dim_index)
    return jnp.concatenate([kept, filler], axis=dim_index)


def cyclic_solve(lower_band, diagonal, upper_band, rights, dim_index):
    length = diagonal.shape[dim_index]
    stride = 1
    while stride < length:
        left_factor = -lower_band / shifted(diagonal, stride, dim_index, 1.0)
        right_factor = -upper_band / shifted(diagonal, -stride, dim_index, 1.0)
        new_diagonal = (
            diagonal
            + left_factor * shifted(upper_band, stride, dim_index, 0.0)
            + right_factor * shifted(lower_band, -stride, dim_index, 0.0)
        )
        new_lower = left_factor * shifted(lower_band, stride, dim_index, 0.0)
        new_upper = right_factor * shifted(upper_band, -stride, dim_index, 0.0)
        rights = tuple(
            (
                column
                + left_factor * shifted(column, stride, dim_index, 0.0)
                + right_factor * shifted(column, -stride, dim_index, 0.0)
                for column in rights
            )
        )
        lower_band, diagonal, upper_band = (new_lower, new_diagonal, new_upper)
        stride = stride * 2
    return tuple((column / diagonal for column in rights))


def complex_product(form, cos_table, sin_table, left_real, left_imag):
    out_real = jnp.einsum(form, cos_table, left_real, precision=highest) - jnp.einsum(
        form, sin_table, left_imag, precision=highest
    )
    out_imag = jnp.einsum(form, cos_table, left_imag, precision=highest) + jnp.einsum(
        form, sin_table, left_real, precision=highest
    )
    return (out_real, out_imag)


def transform(real_part, imag_part, phase_sign, radix):
    batch, length, depth = real_part.shape
    inner_len = length // radix
    outer_idx = jnp.arange(radix, dtype=jnp.int32)
    inner_idx = jnp.arange(inner_len, dtype=jnp.int32)
    first_angle = (
        phase_sign
        * full_turn
        / radix
        * (outer_idx[:, None] * outer_idx[None, :] % radix).astype(jnp.float32)
    )
    twist_angle = (
        phase_sign
        * full_turn
        / length
        * (outer_idx[:, None] * inner_idx[None, :] % length).astype(jnp.float32)
    )
    last_angle = (
        phase_sign
        * full_turn
        / inner_len
        * (inner_idx[:, None] * inner_idx[None, :] % inner_len).astype(jnp.float32)
    )
    shaped_real = real_part.reshape(batch, radix, inner_len, depth)
    shaped_imag = imag_part.reshape(batch, radix, inner_len, depth)
    section_real, section_imag = complex_product(
        "kn,bnmz->bkmz", jnp.cos(first_angle), jnp.sin(first_angle), shaped_real, shaped_imag
    )
    twist_cos = jnp.cos(twist_angle)[None, :, :, None]
    twist_sin = jnp.sin(twist_angle)[None, :, :, None]
    turned_real = section_real * twist_cos - section_imag * twist_sin
    turned_imag = section_real * twist_sin + section_imag * twist_cos
    final_real, final_imag = complex_product(
        "qm,bkmz->bqkz", jnp.cos(last_angle), jnp.sin(last_angle), turned_real, turned_imag
    )
    return (final_real.reshape(batch, length, depth), final_imag.reshape(batch, length, depth))


def on_device(velocity_x, velocity_y, velocity_z, spacing, level_index, plane_index):
    depth = velocity_x.shape[3]
    total_x = velocity_x.shape[2] * lax.axis_size("row")
    groups = lax.axis_size("gz")
    group_id = lax.axis_index("gz")
    levels = spacing.shape[0]
    onehot = (level_index[:, None] == jnp.arange(levels, dtype=jnp.int32)[None, :]).astype(
        jnp.float32
    )
    cell_width = jnp.sum(onehot * spacing[None, :], axis=1)
    lower_band, upper_band = band_coefficients(cell_width)
    own_width = lax.dynamic_slice_in_dim(cell_width, group_id * depth, depth)
    wave_y = plane_index.astype(jnp.float32) * wave_unit
    wall = shifted_2(velocity_z[:, :, :, depth - 1 :], "gz", 1)
    below = jnp.concatenate([wall, velocity_z[:, :, :, : depth - 1]], axis=3).astype(jnp.float32)
    slope = (velocity_z.astype(jnp.float32) - below) / own_width
    wave_col = wave_y[:, None, None]
    across = velocity_y.astype(jnp.float32)
    source_real = -wave_col * across[1] + slope[0]
    source_imag = wave_col * across[0] + slope[1]
    source = jnp.stack([source_real, source_imag]).astype(jnp.bfloat16)
    modes = jnp.arange(total_x, dtype=jnp.int32)
    signed = jnp.where(modes >= total_x // 2, modes - total_x, modes)
    wave_x = signed.astype(jnp.float32) * (full_turn / total_x)
    along = lax.all_to_all(velocity_x, "row", split_axis=1, concat_axis=2, tiled=True)
    spread = lax.all_to_all(source, "row", split_axis=1, concat_axis=2, tiled=True)
    along_real, along_imag = transform(
        along[0].astype(jnp.float32), along[1].astype(jnp.float32), -1.0, RADIX
    )
    src_real, src_imag = transform(
        spread[0].astype(jnp.float32), spread[1].astype(jnp.float32), -1.0, RADIX
    )
    column = wave_x[None, :, None]
    rhs = jnp.stack([src_real - column * along_imag, src_imag + column * along_real])
    local_planes = rhs.shape[1]
    own_wave = lax.dynamic_slice_in_dim(wave_y, lax.axis_index("row") * local_planes, local_planes)
    wave_sq = wave_x[None, :] * wave_x[None, :] + own_wave[:, None] * own_wave[:, None]
    zpos = jnp.arange(depth, dtype=jnp.int32)
    first = zpos == 0
    last = zpos == depth - 1
    edge = first | last
    own_lower = lax.dynamic_slice_in_dim(lower_band, group_id * depth, depth)
    own_upper = lax.dynamic_slice_in_dim(upper_band, group_id * depth, depth)
    block_diag = -(own_lower + own_upper)[None, None, :] - wave_sq[:, :, None]
    block_shape = block_diag.shape
    solved = cyclic_solve(
        jnp.broadcast_to(jnp.where(edge, 0.0, own_lower), block_shape),
        jnp.where(edge, 1.0, block_diag),
        jnp.broadcast_to(jnp.where(edge, 0.0, own_upper), block_shape),
        (
            jnp.where(edge, 0.0, rhs[0]),
            jnp.where(edge, 0.0, rhs[1]),
            jnp.broadcast_to(first.astype(jnp.float32), block_shape),
            jnp.broadcast_to(last.astype(jnp.float32), block_shape),
        ),
        2,
    )
    inner_real, inner_imag, from_first, from_last = solved
    line_ones = jnp.ones(block_shape[:2], jnp.float32)
    head_lower = own_lower[0]
    head_upper = own_upper[0]
    tail_lower = own_lower[depth - 1]
    tail_upper = own_upper[depth - 1]
    packed = jnp.stack(
        [
            line_ones * head_lower,
            tail_lower * from_first[:, :, depth - 2],
            block_diag[:, :, 0] + head_upper * from_first[:, :, 1],
            block_diag[:, :, depth - 1] + tail_lower * from_last[:, :, depth - 2],
            head_upper * from_last[:, :, 1],
            line_ones * tail_upper,
            rhs[0][:, :, 0] - head_upper * inner_real[:, :, 1],
            rhs[0][:, :, depth - 1] - tail_lower * inner_real[:, :, depth - 2],
            rhs[1][:, :, 0] - head_upper * inner_imag[:, :, 1],
            rhs[1][:, :, depth - 1] - tail_lower * inner_imag[:, :, depth - 2],
        ]
    )
    gathered = lax.all_gather(packed, "gz", axis=0, tiled=True).reshape(
        (groups, 10) + block_shape[:2]
    )

    def alternate(start):
        return gathered[:, start : start + 2].reshape((2 * groups,) + block_shape[:2])

    edge_real, edge_imag = cyclic_solve(
        alternate(0), alternate(2), alternate(4), (alternate(6), alternate(8)), 0
    )
    mine_real = lax.dynamic_slice_in_dim(edge_real, 2 * group_id, 2, 0)
    mine_imag = lax.dynamic_slice_in_dim(edge_imag, 2 * group_id, 2, 0)
    real_full = (
        inner_real + from_first * mine_real[0][:, :, None] + from_last * mine_real[1][:, :, None]
    )
    imag_full = (
        inner_imag + from_first * mine_imag[0][:, :, None] + from_last * mine_imag[1][:, :, None]
    )
    spectral = jnp.stack([real_full, imag_full])
    back_real, back_imag = transform(spectral[0], spectral[1], 1.0, RADIX)
    scale = 1.0 / total_x
    pressure_local = jnp.stack([back_real * scale, back_imag * scale])
    return lax.all_to_all(pressure_local, "row", split_axis=2, concat_axis=1, tiled=True)


def solution(mesh):
    placed = (
        P(None, None, "row", "gz"),
        P(None, None, "row", "gz"),
        P(None, None, "row", "gz"),
        P(),
        P(),
        P(),
    )
    return jax.shard_map(
        on_device, mesh=mesh, in_specs=placed, out_specs=P(None, None, "row", "gz"), check_vma=False
    )
```

profile of v0, /device:TPU:0, one launch (start us, length us, event | category | flops | bytes accessed | tf_op | source)
XLA Modules:
  0.0 212.0 jit_solution(10960917810893702241)
XLA Ops:
  2.2 5.9 %collective-permute-start = (bf16[2,8,128,1]{3,2,0,1:T(8,128)(2,1)}, bf16[2,8,128,1]{3,2,0,1:T(8,128)(2,1)}, u32[]{:S(2)}, u32[]{:S(2)}) collective-permute-start(bf16[2,8,128,1]{3,2,0,1:T(8,128)(2,1)} %copy.212), channel_id=1, source_target_pairs={{0,1},{1,2},{2,3},{4,5},{5,6},{6,7},{8,9},{9,10},{10,11},{12,13},{... | collective-permute-start | bytes 12296 | tf_op jit(solution)/shard_map/ppermute | solution.py:19
  9.1 4.2 %all-to-all-start.1 = ((bf16[2,8,128,256]{3,2,0,1:T(8,128)(2,1)}), bf16[2,8,128,256]{3,2,0,1:T(8,128)(2,1)}, u32[]{:S(2)}, u32[]{:S(2)}) async-start(bf16[2,8,128,256]{3,2,0,1:T(8,128)(2,1)} %copy.128), calls=%async_computation.1 | async-start | bytes 2097152 | tf_op jit(solution)/shard_map/all_to_all | solution.py:144
  17.0 1.4 copy_convert_fusion
  23.2 1.7 subtract_divide_fusion
  26.5 2.3 %all-to-all-done.1 = bf16[2,8,128,256]{3,2,0,1:T(8,128)(2,1)} async-done(((bf16[2,8,128,256]{3,2,0,1:T(8,128)(2,1)}), bf16[2,8,128,256]{3,2,0,1:T(8,128)(2,1)}, u32[]{:S(2)}, u32[]{:S(2)}) %all-to-all-start.1) | async-done | bytes 1048608 | tf_op jit(solution)/shard_map/all_to_all | solution.py:144
  28.8 3.7 %all-to-all-start = ((bf16[2,8,128,256]{3,2,0,1:T(8,128)(2,1)}), bf16[2,8,128,256]{3,2,0,1:T(8,128)(2,1)S(1)}, u32[]{:S(2)}, u32[]{:S(2)}) async-start(bf16[2,8,128,256]{3,2,0,1:T(8,128)(2,1)} %pad_maximum_fusion.1), calls=%async_computation | async-start | bytes 2097152 | tf_op jit(solution)/shard_map/all_to_all | solution.py:145
  36.8 10.9 %all-to-all-done = bf16[2,8,128,256]{3,2,0,1:T(8,128)(2,1)S(1)} async-done(((bf16[2,8,128,256]{3,2,0,1:T(8,128)(2,1)}), bf16[2,8,128,256]{3,2,0,1:T(8,128)(2,1)S(1)}, u32[]{:S(2)}, u32[]{:S(2)}) %all-to-all-start) | async-done | bytes 1048608 | tf_op jit(solution)/shard_map/all_to_all | solution.py:145
  51.2 1.5 fusion.40
  52.7 1.5 fusion.36
  54.3 1.5 fusion.9
  55.8 1.7 fusion.34
  57.5 1.5 fusion.30
  59.1 1.5 fusion.8
  60.6 1.5 fusion.7
  62.1 1.5 fusion.6
  63.6 3.8 %broadcast_select_fusion.1 = (f32[1,1024,256]{2,1,0:T(8,128)S(1)}, f32[1,1024,256]{2,1,0:T(8,128)}, f32[1,1024,256]{2,1,0:T(8,128)S(1)}, f32[1,1024,256]{2,1,0:T(8,128)}, f32[1,1024,256]{2,1,0:T(8,128)S(1)}) fusion(pred[256]{0:T(512)(128)(4,1)S(1)} %get-tuple-element.306, f32[1,128,8,256]{3,1,2,0:T(8,128)S(1)} %fusion.6, f32[1024]{0:T(1024)S(1)} %get-tuple-element.309, ...), kind=kLoop, calls=%fused_computation.172 | loop fusion | flops 2097152 | bytes 9446656 | tf_op jit(solution)/shard_map/jit(_where)/select_n | solution.py:171
  68.2 1.8 multiply_add_fusion.8
  75.3 1.4 fusion.271
  76.6 1.7 fusion.282
  78.3 3.5 %multiply_add_fusion.21 = (f32[1,1024,256]{2,1,0:T(8,128)S(1)}, f32[1,1024,256]{2,1,0:T(8,128)S(1)}, f32[1,1024,256]{2,1,0:T(8,128)S(1)}, f32[1,1024,256]{2,1,0:...) fusion(f32[1,1024,256]{2,1,0:T(8,128)S(1)} %get-tuple-element.5, ...), kind=kLoop, calls=%fused_computation.68 | loop fusion | flops 5767168 | bytes 27131904 | tf_op jit(solution)/shard_map/add | solution.py:61
  85.4 1.7 fusion.298
  87.1 3.5 %multiply_add_fusion.20 = (f32[1,1024,256]{2,1,0:T(8,128)S(1)}, f32[1,1024,256]{2,1,0:T(8,128)S(1)}, f32[1,1024,256]{2,1,0:T(8,128)S(1)}, f32[1,1024,256]{2,1,0:...) fusion(f32[1,1024,256]{2,1,0:T(8,128)S(1)} %get-tuple-element.1, ...), kind=kLoop, calls=%fused_computation.67 | loop fusion | flops 5767168 | bytes 27000832 | tf_op jit(solution)/shard_map/add | solution.py:61
  94.1 1.7 fusion.294
  95.8 3.7 %multiply_add_fusion.19 = (f32[1,1024,256]{2,1,0:T(8,128)S(1)}, f32[1,1024,256]{2,1,0:T(8,128)S(1)}, f32[1,1024,256]{2,1,0:T(8,128)S(1)}, f32[1,1024,256]{2,1,0:...) fusion(f32[1,1024,256]{2,1,0:T(8,128)S(1)} %get-tuple-element.1, ...), kind=kLoop, calls=%fused_computation.66 | loop fusion | flops 5767168 | bytes 26738688 | tf_op jit(solution)/shard_map/add | solution.py:61
  103.0 1.7 fusion.290
  104.7 3.5 %multiply_add_fusion.18 = (f32[1,1024,256]{2,1,0:T(8,128)S(1)}, f32[1,1024,256]{2,1,0:T(8,128)S(1)}, f32[1,1024,256]{2,1,0:T(8,128)S(1)}, f32[1,1024,256]{2,1,0:...) fusion(f32[1,1024,256]{2,1,0:T(8,128)S(1)} %get-tuple-element.1, ...), kind=kLoop, calls=%fused_computation.65 | loop fusion | flops 5767168 | bytes 26214400 | tf_op jit(solution)/shard_map/add | solution.py:61
  112.1 4.5 %multiply_add_fusion.17 = (f32[1,1024,256]{2,1,0:T(8,128)S(1)}, f32[1,1024,256]{2,1,0:T(8,128)S(1)}, f32[1,1024,256]{2,1,0:T(8,128)}, f32[1,1024,256]{2,1,0:T(8,...) fusion(f32[1,1024,256]{2,1,0:T(8,128)S(1)} %get-tuple-element.9, ...), kind=kLoop, calls=%fused_computation.64 | loop fusion | flops 5767168 | bytes 25165824 | tf_op jit(solution)/shard_map/add | solution.py:61
  116.6 1.7 fusion.259
  118.3 1.7 fusion.266
  120.0 1.6 fusion.274
  121.6 1.7 fusion.275
  123.3 1.6 fusion.277
  125.0 8.7 %multiply_add_fusion.16 = (f32[1,1024,256]{2,1,0:T(8,128)}, f32[1,1024,256]{2,1,0:T(8,128)}, f32[1,1024,256]{2,1,0:T(8,128)S(1)}, f32[1,1024,256]{2,1,0:T(8,128)...) fusion(f32[1,1024,256]{2,1,0:T(8,128)} %get-tuple-element.87, f32[1,1024,192]{2,1,0:T(8,128)} %get-tuple-element.131, ...), kind=kLoop, calls=%fused_computation.63 | loop fusion | flops 4718592 | bytes 20447232 | tf_op jit(solution)/shard_map/add | solution.py:61
  139.5 2.1 fusion.43
  142.8 2.1 fusion.47
  144.9 2.6 %fusion.50 = (f32[1024]{0:T(1024)S(1)}, f32[1024]{0:T(1024)S(1)}, f32[1024]{0:T(1024)S(1)}, f32[1024]{0:T(1024)S(1)}) fusion(f32[1,1024,256]{2,1,0:T(8,128)S(1)} %get-tuple-element.65, f32[]{:T(128)} %bitcast.37, f32[]{:T(128)} %bitcast.36, f32[1,1024,256]{2,1,0:T(8,128)S(1)} %copy-done.8, f32[1,1024,256]{2,1,0:T(8,128)S(1)} %get-tuple-element.63), kind=kLoop, calls=%fused_computation.155 | loop fusion | flops 6144 | bytes 40968 | tf_op jit(solution)/shard_map/mul | solution.py:189
  148.2 13.5 %all_gather.3 = f32[40,1,1024]{2,1,0:T(1,128)S(1)} all-gather(f32[10,1,1024]{2,1,0:T(1,128)S(1)} %constant_dynamic-update-slice_fusion), channel_id=1, replica_groups=mesh['row'=8,'gz'=4] {'gz'}, dimensions={0}, use_global_device_ids=true | all-gather | bytes 204800 | tf_op jit(solution)/shard_map/all_gather | solution.py:197
  164.1 1.6 fusion.24
  165.7 1.6 fusion.28
  167.3 1.6 fusion.4
  169.0 2.1 subtract_bitcast_fusion
  171.1 1.5 fusion.22
  172.6 1.5 fusion.18
  174.1 1.5 fusion.3
  176.6 1.5 fusion.1
  178.9 2.2 %copy.152 = f32[2,1,1024,256]{3,1,0,2:T(1,128)S(1)} copy(f32[2,1,1024,256]{3,2,1,0:T(8,128)S(1)} %pad_maximum_fusion) | data formatting | bytes 4194304 | tf_op jit(solution)/shard_map/stack | solution.py:218
  181.0 29.0 %all_to_all.30 = f32[2,1,1024,256]{3,1,0,2:T(1,128)S(1)} all-to-all(f32[2,1,1024,256]{3,1,0,2:T(1,128)S(1)} %copy.152), channel_id=1, replica_groups=mesh['row'=8,'gz'=4] {'row'}, dimensions={2} | all-to-all | bytes 4194304 | tf_op jit(solution)/shard_map/all_to_all | solution.py:219
  210.0 1.5 copy.154
  (171 shorter events, 51.5 us)
Async XLA Ops:
  0.0 8.1 %copy-start.11 = (bf16[2,8,128,256]{3,2,1,0:T(8,128)(2,1)S(1)}, bf16[2,8,128,256]{3,2,1,0:T(8,128)(2,1)}, u32[]{:S(2)}) copy-start(bf16[2,8,128,256]{3,2,1,0:T(8,128)(2,1)} %param.6) | copy-start | bytes 3145732
  2.2 11.3 %copy-start.14 = (s32[1024]{0:T(1024)S(1)}, s32[1024]{0:T(1024)}, u32[]{:S(2)}) copy-start(s32[1024]{0:T(1024)} %param.10) | copy-start | bytes 12292
  2.2 11.3 %copy-start.15 = (f32[64]{0:T(128)S(1)}, f32[64]{0:T(128)}, u32[]{:S(2)}) copy-start(f32[64]{0:T(128)} %param.9) | copy-start | bytes 772
  2.2 14.8 %copy-start.16 = (s32[8]{0:T(128)S(1)}, s32[8]{0:T(128)}, u32[]{:S(2)}) copy-start(s32[8]{0:T(128)} %param.11) | copy-start | bytes 100
  2.2 21.0 %collective-permute-start = (bf16[2,8,128,1]{3,2,0,1:T(8,128)(2,1)}, bf16[2,8,128,1]{3,2,0,1:T(8,128)(2,1)}, u32[]{:S(2)}, u32[]{:S(2)}) collective-permute-start(bf16[2,8,128,1]{3,2,0,1:T(8,128)(2,1)} %copy.212), channel_id=1, source_target_pairs={{0,1},{1,2},{2,3},{4,5},{5,6},{6,7},{8,9},{9,10},{10,11},{12,13},{... | collective-permute-start | bytes 12296 | tf_op jit(solution)/shard_map/ppermute | solution.py:19
  9.1 19.6 %all-to-all-start.1 = ((bf16[2,8,128,256]{3,2,0,1:T(8,128)(2,1)}), bf16[2,8,128,256]{3,2,0,1:T(8,128)(2,1)}, u32[]{:S(2)}, u32[]{:S(2)}) async-start(bf16[2,8,128,256]{3,2,0,1:T(8,128)(2,1)} %copy.128), calls=%async_computation.1 | async-start | bytes 2097152 | tf_op jit(solution)/shard_map/all_to_all | solution.py:144
  13.4 9.9 %copy-start.7 = (bf16[2,8,128,256]{3,2,1,0:T(8,128)(2,1)S(1)}, bf16[2,8,128,256]{3,2,1,0:T(8,128)(2,1)}, u32[]{:S(2)}) copy-start(bf16[2,8,128,256]{3,2,1,0:T(8,128)(2,1)} %param.8) | copy-start | bytes 3145732
  28.8 18.9 %all-to-all-start = ((bf16[2,8,128,256]{3,2,0,1:T(8,128)(2,1)}), bf16[2,8,128,256]{3,2,0,1:T(8,128)(2,1)S(1)}, u32[]{:S(2)}, u32[]{:S(2)}) async-start(bf16[2,8,128,256]{3,2,0,1:T(8,128)(2,1)} %pad_maximum_fusion.1), calls=%async_computation | async-start | bytes 2097152 | tf_op jit(solution)/shard_map/all_to_all | solution.py:145
  116.5 1.7 copy-start
  133.7 1.5 copy-start.4
  135.0 1.3 copy-start.2
  135.1 1.5 copy-start.1
  135.2 1.7 copy-start.3
  136.3 1.4 copy-start.6
  136.9 1.3 copy-start.5
  138.2 1.2 copy-start.10
  141.5 1.2 copy-start.9
  142.2 2.7 %copy-start.8 = (f32[1,1024,256]{2,1,0:T(8,128)S(1)}, f32[1,1024,256]{2,1,0:T(8,128)}, u32[]{:S(2)}) copy-start(f32[1,1024,256]{2,1,0:T(8,128)} %get-tuple-element.274) | copy-start | bytes 3145732
  167.3 1.6 copy-start.12
  167.3 1.6 copy-start.13
where the time goes:
time: 215 us; the launch traced here: 212 us
  local copies, waits for them, and re-layouts  54.8 us (25%)
  other arithmetic  53.4 us (25%)
  blocking collectives  42.5 us (20%)
  matrix products  31.7 us (15%)
  starting transfers between devices  13.9 us (6%)
  waiting for transfers between devices  13.2 us (6%)
  between operations  2.52 us (1%)
    add x11, other arithmetic, cyclic_solve(): column + left_factor * shifted(column, stride, dim_index, 0.0)  31.7 us
    all_to_all x1, blocking collectives, on_device(): lax.all_to_all(pressure_local, 'row', split_axis=2, concat_axis=1, tiled=...  29 us
    slice x47, local copies, waits for them, and re-layouts, shifted(): kept = lax.slice_in_dim(values, 0, length - offset, axis=dim_index)  27.3 us
    all_gather x1, blocking collectives, on_device(): lax.all_gather(packed, 'gz', axis=0, tiled=True)  13.5 us
    all_to_all x1, waiting for transfers between devices, on_device(): lax.all_to_all(source, 'row', split_axis=1, concat_axis=2, tiled=True)  10.9 us
    dot_general x6, matrix products, complex_product(): jnp.einsum(form, sin_table, left_imag, precision=highest)  8.69 us
    slice x24, local copies, waits for them, and re-layouts, shifted(): kept = lax.slice_in_dim(values, -offset, length, axis=dim_index)  7.87 us
    dot_general x6, matrix products, complex_product(): jnp.einsum(form, cos_table, left_imag, precision=highest)  7.81 us
  transfers between devices with their start and end apart: 3, of which 2 were waited for; matrix products, arithmetic and copies ran while one was open for 8% of the time, Pallas kernels for 0%

commit v1 on v0

v1 whole, which is shorter than its diff:
```python
import functools
import math

import jax
import jax.numpy as jnp
import numpy as np
from jax import lax
from jax.experimental import pallas as pl
from jax.experimental.pallas import tpu as pltpu
from jax.sharding import PartitionSpec as P

RADIX = 8
LANES = 128

full_turn = 2.0 * math.pi
wave_unit = 2.0 * math.pi / 2048.0


def phase_tables(total_x):
    inner = total_x // RADIX
    k1 = np.arange(RADIX)[:, None, None]
    m = np.arange(inner)[None, :, None]
    k2 = np.arange(inner)[None, None, :]
    angle = -full_turn * ((m * (k1 + RADIX * k2)) % total_x) / total_x
    cos, sin = np.cos(angle), np.sin(angle)
    table = np.concatenate(
        [np.concatenate([cos, sin], axis=2), np.concatenate([-sin, cos], axis=2)], axis=1
    )
    high = table.astype(jnp.bfloat16)
    low = (table - high.astype(np.float64)).astype(jnp.bfloat16)
    return high, low


def radix_eight(re, im, sign):
    half = math.sqrt(0.5)
    add = lambda a, b: (a[0] + b[0], a[1] + b[1])
    sub = lambda a, b: (a[0] - b[0], a[1] - b[1])
    turn = lambda a: (-sign * a[1], sign * a[0])
    x = list(zip(re, im))
    even = [add(x[j], x[j + 4]) for j in range(4)]
    odd = [sub(x[j], x[j + 4]) for j in range(4)]
    a, b = odd[1]
    odd[1] = (half * (a - sign * b), half * (b + sign * a))
    odd[2] = turn(odd[2])
    a, b = odd[3]
    odd[3] = (half * (-a - sign * b), half * (sign * a - b))

    def four(v):
        t0, t1 = add(v[0], v[2]), sub(v[0], v[2])
        t2, t3 = add(v[1], v[3]), turn(sub(v[1], v[3]))
        return [add(t0, t2), add(t1, t3), sub(t0, t2), sub(t1, t3)]

    e, o = four(even), four(odd)
    out = [e[0], o[0], e[1], o[1], e[2], o[2], e[3], o[3]]
    return [v[0] for v in out], [v[1] for v in out]


def split(value):
    high = value.astype(jnp.bfloat16)
    return high, (value - high.astype(jnp.float32)).astype(jnp.bfloat16)


def kernel(
    rows, groups,
    vx, vy_hbm, vz_hbm, wh_hbm, wl_hbm, level_row, spacing, level, plane,
    out,
    vy, vz, wh, wl, wall_out, wall_in, src, got_u, got_s,
    yh, yl, rhs_re, rhs_im, qq, lq, uq, from_lo, from_hi, coef, edge, solved, spec, back,
    load_sem, own_sem, u_send, u_recv, s_send, s_recv, w_send, w_recv,
    c_send, c_recv, e_send, e_recv, p_send, p_recv,
):
    me = lax.axis_index("row")
    gz = lax.axis_index("gz")
    planes, part, depth = vx.shape[1:]
    total_x = part * rows
    inner = total_x // RADIX
    total_z = level.shape[0]
    levels = spacing.shape[0]
    f32 = jnp.float32

    loads = [
        pltpu.make_async_copy(vz_hbm, vz, load_sem.at[0]),
        pltpu.make_async_copy(vy_hbm, vy, load_sem.at[1]),
        pltpu.make_async_copy(wh_hbm, wh, load_sem.at[2]),
        pltpu.make_async_copy(wl_hbm, wl, load_sem.at[3]),
    ]
    for load in loads:
        load.start()
    mine = pl.ds(pl.multiple_of(me * part, part), part)
    own_u = pltpu.make_async_copy(vx.at[:, me], got_u.at[:, mine, :], own_sem.at[0])
    own_u.start()

    barrier = pltpu.get_barrier_semaphore()
    for i in range(1, rows):
        pl.semaphore_signal(
            barrier, inc=1, device_id={"row": lax.rem(me + i, rows)},
            device_id_type=pl.DeviceIdType.MESH,
        )
    for i in range(1, groups):
        pl.semaphore_signal(
            barrier, inc=1, device_id={"gz": lax.rem(gz + i, groups)},
            device_id_type=pl.DeviceIdType.MESH,
        )
    pl.semaphore_wait(barrier, rows + groups - 2)

    def to_row(source, target, send, recv, i):
        return pltpu.make_async_remote_copy(
            src_ref=source, dst_ref=target, send_sem=send, recv_sem=recv,
            device_id={"row": lax.rem(me + i, rows)}, device_id_type=pl.DeviceIdType.MESH,
        )

    def to_group(source, target, send, recv, i):
        return pltpu.make_async_remote_copy(
            src_ref=source, dst_ref=target, send_sem=send, recv_sem=recv,
            device_id={"gz": lax.rem(gz + i, groups)}, device_id_type=pl.DeviceIdType.MESH,
        )

    sends_u = []
    for i in range(1, rows):
        copy = to_row(
            vx.at[:, lax.rem(me + i, rows)], got_u.at[:, mine, :], u_send.at[i], u_recv.at[i], i
        )
        copy.start()
        sends_u.append(copy)

    lane_small = lax.broadcasted_iota(jnp.int32, (part, LANES), 1)
    loads[0].wait()
    packed = jnp.zeros((part, LANES), f32)
    for c in range(2):
        for p in range(planes):
            slot = c * planes + p
            tile = vz[c, p, :, depth - LANES :].astype(f32)
            packed = jnp.where(lane_small == slot, pltpu.roll(tile, (slot + 1) % LANES, 1), packed)
    wall_out[...] = packed.astype(jnp.bfloat16)
    wall_copy = to_group(wall_out, wall_in, w_send, w_recv, 1)

    @pl.when(gz < groups - 1)
    def _():
        wall_copy.start()

    base = gz * depth
    own_level = level_row[:, pl.ds(pl.multiple_of(base, LANES), depth)]
    width = jnp.zeros((1, depth), f32)
    for n in range(levels):
        width = jnp.where(own_level == n, spacing[n], width)
    loads[1].wait()

    @pl.when(gz > 0)
    def _():
        wall_copy.wait_recv()

    @pl.when(gz == 0)
    def _():
        wall_in[...] = jnp.zeros_like(wall_in)

    first_lane = lax.broadcasted_iota(jnp.int32, (part, depth), 1) == 0

    def slope_of(c, p):
        values = vz[c, p].astype(f32)
        slot = c * planes + p
        turned = pltpu.roll(wall_in[...].astype(f32), lax.rem(LANES - slot, LANES), 1)
        if depth > LANES:
            turned = jnp.concatenate([turned] * (depth // LANES), axis=1)
        below = jnp.where(first_lane, turned, pltpu.roll(values, 1, 1))
        return (values - below) / width

    def make_source(i, carry):
        p = lax.rem(me + i, rows)
        wave = jnp.full((1, depth), plane[p], jnp.int32).astype(f32) * wave_unit
        src[p, 0] = (-wave * vy[1, p].astype(f32) + slope_of(0, p)).astype(jnp.bfloat16)
        src[p, 1] = (wave * vy[0, p].astype(f32) + slope_of(1, p)).astype(jnp.bfloat16)

        @pl.when(i > 0)
        def _():
            to_row(src.at[p], got_s.at[:, mine, :], s_send.at[i], s_recv.at[i], i).start()

        return carry

    lax.fori_loop(1, rows, make_source, 0)
    make_source(0, 0)
    own_s = pltpu.make_async_copy(src.at[me], got_s.at[:, mine, :], own_sem.at[1])
    own_s.start()

    tile = (RADIX, inner)
    k1s = lax.broadcasted_iota(jnp.int32, tile, 0)
    k2s = lax.broadcasted_iota(jnp.int32, tile, 1)
    modes = k1s + RADIX * k2s
    wave_x = jnp.where(modes >= total_x // 2, modes - total_x, modes).astype(f32) * (
        full_turn / total_x
    )
    wave_y = jnp.full(tile, plane[me], jnp.int32).astype(f32) * wave_unit
    wave_sq = wave_x * wave_x + wave_y * wave_y

    def width_at(j):
        return jnp.full(tile, spacing[level[jnp.clip(j, 0, total_z - 1)]], f32)

    def factor(j, carry):
        excess, h_prev, h_now, homog = carry
        at = base + j
        h_next = width_at(at + 1)
        flag_lo = jnp.where(at > 0, 1.0, 0.0).astype(f32)
        flag_hi = jnp.where(at < total_z - 1, 1.0, 0.0).astype(f32)
        lower = flag_lo / (0.5 * (h_prev + h_now) * h_now)
        upper = flag_hi / (0.5 * (h_now + h_next) * h_now)
        s = wave_sq + lower * excess
        q = 1.0 / (upper + s)
        homog = lower * q * homog
        rows_j = pl.ds(pl.multiple_of(j * RADIX, RADIX), RADIX)
        qq[rows_j, :] = q
        lq[rows_j, :] = lower * q
        uq[rows_j, :] = upper * q
        from_lo[rows_j, :] = homog
        return s * q, h_now, h_next, homog

    one = jnp.ones(tile, f32)
    lax.fori_loop(0, depth, factor, (one, width_at(base - 1), width_at(base), one))

    def factor_back(t, carry):
        lo, hi = carry
        j = depth - 1 - t
        rows_j = pl.ds(pl.multiple_of(j * RADIX, RADIX), RADIX)
        ratio = uq[rows_j, :]
        lo = from_lo[rows_j, :] + ratio * lo
        hi = ratio * hi
        from_lo[rows_j, :] = lo
        from_hi[rows_j, :] = hi
        return lo, hi

    lax.fori_loop(0, depth, factor_back, (jnp.zeros(tile, f32), one))
    top = (depth - 1) * RADIX
    coef[gz, 0] = from_lo[0:RADIX, :]
    coef[gz, 1] = from_hi[0:RADIX, :]
    coef[gz, 2] = from_lo[top : top + RADIX, :]
    coef[gz, 3] = from_hi[top : top + RADIX, :]
    sends_c = []
    for i in range(1, groups):
        copy = to_group(coef.at[gz], coef.at[gz], c_send.at[i], c_recv.at[i], i)
        copy.start()
        sends_c.append(copy)

    step = 16

    def first_stage(field):
        def body(t, carry):
            at = pl.multiple_of(t * step, step)
            for lane in range(0, depth, LANES):
                cols = pl.ds(lane, LANES)
                re = [field[0, pl.ds(r * inner + at, step), cols].astype(f32) for r in range(RADIX)]
                im = [field[1, pl.ds(r * inner + at, step), cols].astype(f32) for r in range(RADIX)]
                re, im = radix_eight(re, im, -1.0)
                for k in range(RADIX):
                    h, l = split(re[k])
                    yh[k, pl.ds(at, step), cols] = h
                    yl[k, pl.ds(at, step), cols] = l
                    h, l = split(im[k])
                    yh[k, pl.ds(inner + at, step), cols] = h
                    yl[k, pl.ds(inner + at, step), cols] = l
            return carry

        lax.fori_loop(0, inner // step, body, 0)

    over_rows = (((0,), (0,)), ((), ()))
    over_last = (((1,), (1,)), ((), ()))

    def dot(a, b, dims):
        return lax.dot_general(a, b, dims, preferred_element_type=f32)

    def second_stage(combine):
        def body(k, carry):
            h, l, a, b = yh[k], yl[k], wh[k], wl[k]
            hat = dot(h, a, over_rows) + dot(h, b, over_rows) + dot(l, a, over_rows)
            combine(k, hat[:, :inner], hat[:, inner:])
            return carry

        lax.fori_loop(0, RADIX, body, 0)

    def put_along(k, re, im):
        number = k + RADIX * lax.broadcasted_iota(jnp.int32, (1, inner), 1)
        column = jnp.where(number >= total_x // 2, number - total_x, number).astype(f32) * (
            full_turn / total_x
        )
        where = pl.ds(k, depth, stride=RADIX)
        rhs_re[where, :] = -column * im
        rhs_im[where, :] = column * re

    def put_source(k, re, im):
        where = pl.ds(k, depth, stride=RADIX)
        rhs_re[where, :] = rhs_re[where, :] + re
        rhs_im[where, :] = rhs_im[where, :] + im

    own_u.wait()
    for copy in sends_u:
        copy.wait()
    for load in loads[2:]:
        load.wait()
    first_stage(got_u)
    second_stage(put_along)
    own_s.wait()
    for i in range(1, rows):
        to_row(
            src.at[lax.rem(me + i, rows)], got_s.at[:, mine, :], s_send.at[i], s_recv.at[i], i
        ).wait()
    first_stage(got_s)
    second_stage(put_source)

    def sweep(j, carry):
        re, im = carry
        rows_j = pl.ds(pl.multiple_of(j * RADIX, RADIX), RADIX)
        q, low = qq[rows_j, :], lq[rows_j, :]
        re = low * re - q * rhs_re[rows_j, :]
        im = low * im - q * rhs_im[rows_j, :]
        rhs_re[rows_j, :] = re
        rhs_im[rows_j, :] = im
        return re, im

    def sweep_back(t, carry):
        re, im = carry
        rows_j = pl.ds(pl.multiple_of((depth - 1 - t) * RADIX, RADIX), RADIX)
        ratio = uq[rows_j, :]
        re = rhs_re[rows_j, :] + ratio * re
        im = rhs_im[rows_j, :] + ratio * im
        rhs_re[rows_j, :] = re
        rhs_im[rows_j, :] = im
        return re, im

    zero = jnp.zeros(tile, f32)
    lax.fori_loop(0, depth, sweep, (zero, zero), unroll=4)
    lax.fori_loop(0, depth, sweep_back, (zero, zero), unroll=4)

    edge[gz, 0] = rhs_re[0:RADIX, :]
    edge[gz, 1] = rhs_re[top : top + RADIX, :]
    edge[gz, 2] = rhs_im[0:RADIX, :]
    edge[gz, 3] = rhs_im[top : top + RADIX, :]
    sends_e = []
    for i in range(1, groups):
        copy = to_group(edge.at[gz], edge.at[gz], e_send.at[i], e_recv.at[i], i)
        copy.start()
        sends_e.append(copy)
    for copy in sends_c:
        copy.wait()
    for copy in sends_e:
        copy.wait()
    if groups > 1 or True:
        last_const, last_ratio = [(zero, zero)], [zero]
        head_const, head_ratio = [], []
        for b in range(groups):
            a0, b0, a1, b1 = (coef[b, n] for n in range(4))
            inv = 1.0 / (1.0 - a0 * last_ratio[b])
            ratio = b0 * inv
            head_ratio.append(ratio)
            heads, lasts = [], []
            for part_of in range(2):
                prev = last_const[b][part_of]
                head = (edge[b, 2 * part_of] + a0 * prev) * inv
                heads.append(head)
                lasts.append(edge[b, 2 * part_of + 1] + a1 * (prev + last_ratio[b] * head))
            head_const.append(heads)
            last_const.append(lasts)
            last_ratio.append(a1 * last_ratio[b] * ratio + b1)
        for part_of in range(2):
            following = zero
            heads = [zero] * (groups + 1)
            for b in reversed(range(groups)):
                heads[b] = head_const[b][part_of] + head_ratio[b] * heads[b + 1]
            for b in range(groups):
                below = last_const[b][part_of] + last_ratio[b] * heads[b]
                solved[b, part_of, 0] = below
                solved[b, part_of, 1] = heads[b + 1]
    below_re, above_re = solved[gz, 0, 0], solved[gz, 0, 1]
    below_im, above_im = solved[gz, 1, 0], solved[gz, 1, 1]

    def join(j, carry):
        rows_j = pl.ds(pl.multiple_of(j * RADIX, RADIX), RADIX)
        lo, hi = from_lo[rows_j, :], from_hi[rows_j, :]
        rhs_re[rows_j, :] = rhs_re[rows_j, :] + lo * below_re + hi * above_re
        rhs_im[rows_j, :] = rhs_im[rows_j, :] + lo * below_im + hi * above_im
        return carry

    scale = 1.0 / total_x
    sends_p = []
    own_p = []
    for z in range(depth // LANES):
        start = z * LANES
        cols = pl.ds(start, LANES)
        lax.fori_loop(start, start + LANES, join, 0, unroll=4)

        def inverse(k, carry):
            where = pl.ds(start * RADIX + k, LANES, stride=RADIX)
            line = jnp.concatenate([rhs_re[where, :], rhs_im[where, :]], axis=1)
            h, l = split(line)
            a, b = wh[k], wl[k]
            spec[k] = dot(a, h, over_last) + dot(b, h, over_last) + dot(a, l, over_last)
            return carry

        lax.fori_loop(0, RADIX, inverse, 0)

        def last_stage(t, carry):
            at = pl.multiple_of(t * 8, 8)
            re = [spec[k, pl.ds(at, 8), :] for k in range(RADIX)]
            im = [spec[k, pl.ds(inner + at, 8), :] for k in range(RADIX)]
            re, im = radix_eight(re, im, 1.0)
            for r in range(RADIX):
                back[0, pl.ds(r * inner + at, 8), cols] = re[r] * scale
                back[1, pl.ds(r * inner + at, 8), cols] = im[r] * scale
            return carry

        lax.fori_loop(0, inner // 8, last_stage, 0, unroll=2)
        for i in range(1, rows):
            theirs = pl.ds(pl.multiple_of(lax.rem(me + i, rows) * part, part), part)
            copy = to_row(
                back.at[:, theirs, cols], out.at[:, me, :, cols],
                p_send.at[z, i], p_recv.at[z, i], i,
            )
            copy.start()
            sends_p.append(copy)
        copy = pltpu.make_async_copy(
            back.at[:, mine, cols], out.at[:, me, :, cols], own_sem.at[2 + z]
        )
        copy.start()
        own_p.append(copy)
    for copy in own_p + sends_p:
        copy.wait()

    @pl.when(gz < groups - 1)
    def _():
        wall_copy.wait_send()


def on_device(rows, groups, velocity_x, velocity_y, velocity_z, spacing, level_index, plane_index):
    planes, part, depth = velocity_x.shape[1:]
    total_x = part * rows
    inner = total_x // RADIX
    assert planes == rows and depth % LANES == 0 and inner % LANES == 0
    high, low = phase_tables(total_x)
    bf16, f32 = jnp.bfloat16, jnp.float32
    vmem = pltpu.VMEM
    lines = (depth * RADIX, inner)
    dma = pltpu.SemaphoreType.DMA
    hbm = pl.BlockSpec(memory_space=pl.ANY)
    smem = pl.BlockSpec(memory_space=pltpu.SMEM)
    return pl.pallas_call(
        functools.partial(kernel, rows, groups),
        out_shape=jax.ShapeDtypeStruct(velocity_x.shape, f32),
        in_specs=[hbm] * 5 + [pl.BlockSpec(memory_space=pltpu.VMEM), smem, smem, smem],
        out_specs=hbm,
        scratch_shapes=[
            vmem(velocity_y.shape, bf16),
            vmem(velocity_z.shape, bf16),
            vmem(high.shape, bf16),
            vmem(high.shape, bf16),
            vmem((part, LANES), bf16),
            vmem((part, LANES), bf16),
            vmem((planes, 2, part, depth), bf16),
            vmem((2, total_x, depth), bf16),
            vmem((2, total_x, depth), bf16),
            vmem((RADIX, 2 * inner, depth), bf16),
            vmem((RADIX, 2 * inner, depth), bf16),
        ]
        + [vmem(lines, f32)] * 7
        + [
            vmem((groups, 4, RADIX, inner), f32),
            vmem((groups, 4, RADIX, inner), f32),
            vmem((groups, 2, 2, RADIX, inner), f32),
            vmem((RADIX, 2 * inner, LANES), f32),
            vmem((2, total_x, depth), f32),
            dma((4,)),
            dma((2 + depth // LANES,)),
            dma((rows,)), dma((rows,)), dma((rows,)), dma((rows,)),
            dma, dma,
            dma((groups,)), dma((groups,)), dma((groups,)), dma((groups,)),
            dma((depth // LANES, rows)), dma((depth // LANES, rows)),
        ],
        compiler_params=pltpu.CompilerParams(
            collective_id=0, has_side_effects=True, vmem_limit_bytes=56 * 1024 * 1024
        ),
    )(
        velocity_x, velocity_y, velocity_z, jnp.asarray(high), jnp.asarray(low),
        level_index.reshape(1, -1), spacing, level_index, plane_index,
    )


def solution(mesh):
    placed = (
        P(None, None, "row", "gz"),
        P(None, None, "row", "gz"),
        P(None, None, "row", "gz"),
        P(),
        P(),
        P(),
    )
    body = functools.partial(on_device, mesh.shape["row"], mesh.shape["gz"])
    return jax.shard_map(
        body, mesh=mesh, in_specs=placed, out_specs=P(None, None, "row", "gz"), check_vma=False
    )
```

time: 215 us -> 69.8 us (0.32)
  Pallas kernels: 0 us -> 65.4 us
  other arithmetic: 53.4 us -> 0 us
  local copies, waits for them, and re-layouts: 54.8 us -> 3.1 us
  blocking collectives: 42.5 us -> 0 us
  matrix products: 31.7 us -> 0 us
  starting transfers between devices: 13.9 us -> 0 us
  waiting for transfers between devices: 13.2 us -> 0 us
  between operations: 2.52 us -> 0.01 us
    pallas_call x0 -> x1, Pallas kernels: none -> 65.4 us  [on_device(): pl.pallas_call(functools.partial(kernel, rows, groups), out_shape=jax.Sha...]
    slice x81 -> x0, local copies, waits for them, and re-layouts: 39.7 us -> none  [the longest x47 27.3 us: shifted(): kept = lax.slice_in_dim(values, 0, length - offset, axis=dim_index)]
    add x20 -> x0, other arithmetic: 35.2 us -> none  [the longest x11 31.7 us: cyclic_solve(): column + left_factor * shifted(column, stride, dim_index, 0.0)]
    dot_general x24 -> x0, matrix products: 31.7 us -> none  [the longest x6 8.69 us: complex_product(): jnp.einsum(form, sin_table, left_imag, precision=highest)]
    all_to_all x1 -> x0, blocking collectives: 29 us -> none  [on_device(): lax.all_to_all(pressure_local, 'row', split_axis=2, concat_axis=1, tiled=...]
    all_gather x1 -> x0, blocking collectives: 13.5 us -> none  [on_device(): lax.all_gather(packed, 'gz', axis=0, tiled=True)]
    all_to_all x2 -> x0, waiting for transfers between devices: 13.2 us -> none  [the longest x1 10.9 us: on_device(): lax.all_to_all(source, 'row', split_axis=1, concat_axis=2, tiled=True)]
    all_to_all x2 -> x0, starting transfers between devices: 7.98 us -> none  [the longest x1 4.25 us: on_device(): lax.all_to_all(velocity_x, 'row', split_axis=1, concat_axis=2, tiled=True)]
  transfers between devices with their start and end apart: 3 -> 0, of which waited for: 2 -> 0; matrix products, arithmetic and copies ran while one was open for 8% -> 0% of each run, Pallas kernels for 0% -> 0%
where the time goes in v1:
time: 69.8 us; the launch traced here: 68.5 us
  Pallas kernels  65.4 us (94%)
  local copies, waits for them, and re-layouts  3.1 us (4%)
    pallas_call x1, Pallas kernels, on_device(): pl.pallas_call(functools.partial(kernel, rows, groups), out_shape=jax.Sha...  65.4 us
    unnamed x1, local copies, waits for them, and re-layouts  3.1 us

profile of v1, /device:TPU:0, one launch (start us, length us, event | category | flops | bytes accessed | tf_op | source)
XLA Modules:
  0.0 68.5 jit_solution(15323404940870218230)
XLA Ops:
  0.0 65.4 %shard_map.82 = f32[2,8,128,256]{3,2,1,0:T(8,128)} custom-call(bf16[2,8,128,256]{3,2,1,0:T(8,128)(2,1)} %vx.1, bf16[2,8,128,256]{3,2,1,0:T(8,128)(2,1)} %vy_hbm.1, bf16[2,8,128,256]{3,2,1,0:T(8,128)(2,1)} %vz_hbm.1, bf16[8,256,256]{2,1,0:T(8,128)(2,1)} %constant.4.clone.wh_hbm, bf16[8,256,256]{2,1,0:T(8,128)(2,1)} %constant.5.clone.wl_hbm, ...), custom_call_target="tpu_custom_call" | custom-call | tf_op jit(solution)/shard_map/pallas_call | solution.py:441
  65.4 3.1 %copy.10 = f32[2,8,128,256]{3,2,1,0:T(8,128)} copy(f32[2,8,128,256]{3,2,1,0:T(8,128)} %shard_map.82) | data formatting | bytes 4194304

commit v2 on v1

--- a/solution.py
+++ b/solution.py
@@ -213,7 +213,7 @@
         return s * q, h_now, h_next, homog
 
     one = jnp.ones(tile, f32)
-    lax.fori_loop(0, depth, factor, (one, width_at(base - 1), width_at(base), one))
+    lax.fori_loop(0, depth, factor, (one, width_at(base - 1), width_at(base), one), unroll=4)
 
     def factor_back(t, carry):
         lo, hi = carry
@@ -226,7 +226,7 @@
         from_hi[rows_j, :] = hi
         return lo, hi
 
-    lax.fori_loop(0, depth, factor_back, (jnp.zeros(tile, f32), one))
+    lax.fori_loop(0, depth, factor_back, (jnp.zeros(tile, f32), one), unroll=4)
     top = (depth - 1) * RADIX
     coef[gz, 0] = from_lo[0:RADIX, :]
     coef[gz, 1] = from_hi[0:RADIX, :]
@@ -340,7 +340,7 @@
         copy.wait()
     for copy in sends_e:
         copy.wait()
-    if groups > 1 or True:
+    if True:
         last_const, last_ratio = [(zero, zero)], [zero]
         head_const, head_ratio = [], []
         for b in range(groups):
@@ -395,16 +395,16 @@
         lax.fori_loop(0, RADIX, inverse, 0)
 
         def last_stage(t, carry):
-            at = pl.multiple_of(t * 8, 8)
-            re = [spec[k, pl.ds(at, 8), :] for k in range(RADIX)]
-            im = [spec[k, pl.ds(inner + at, 8), :] for k in range(RADIX)]
+            at = pl.multiple_of(t * step, step)
+            re = [spec[k, pl.ds(at, step), :] for k in range(RADIX)]
+            im = [spec[k, pl.ds(inner + at, step), :] for k in range(RADIX)]
             re, im = radix_eight(re, im, 1.0)
             for r in range(RADIX):
-                back[0, pl.ds(r * inner + at, 8), cols] = re[r] * scale
-                back[1, pl.ds(r * inner + at, 8), cols] = im[r] * scale
+                back[0, pl.ds(r * inner + at, step), cols] = (re[r] * scale).astype(jnp.bfloat16)
+                back[1, pl.ds(r * inner + at, step), cols] = (im[r] * scale).astype(jnp.bfloat16)
             return carry
 
-        lax.fori_loop(0, inner // 8, last_stage, 0, unroll=2)
+        lax.fori_loop(0, inner // step, last_stage, 0)
         for i in range(1, rows):
             theirs = pl.ds(pl.multiple_of(lax.rem(me + i, rows) * part, part), part)
             copy = to_row(
@@ -438,9 +438,9 @@
     dma = pltpu.SemaphoreType.DMA
     hbm = pl.BlockSpec(memory_space=pl.ANY)
     smem = pl.BlockSpec(memory_space=pltpu.SMEM)
-    return pl.pallas_call(
+    received = pl.pallas_call(
         functools.partial(kernel, rows, groups),
-        out_shape=jax.ShapeDtypeStruct(velocity_x.shape, f32),
+        out_shape=jax.ShapeDtypeStruct(velocity_x.shape, bf16),
         in_specs=[hbm] * 5 + [pl.BlockSpec(memory_space=pltpu.VMEM), smem, smem, smem],
         out_specs=hbm,
         scratch_shapes=[
@@ -462,7 +462,7 @@
             vmem((groups, 4, RADIX, inner), f32),
             vmem((groups, 2, 2, RADIX, inner), f32),
             vmem((RADIX, 2 * inner, LANES), f32),
-            vmem((2, total_x, depth), f32),
+            vmem((2, total_x, depth), bf16),
             dma((4,)),
             dma((2 + depth // LANES,)),
             dma((rows,)), dma((rows,)), dma((rows,)), dma((rows,)),
@@ -477,6 +477,7 @@
         velocity_x, velocity_y, velocity_z, jnp.asarray(high), jnp.asarray(low),
         level_index.reshape(1, -1), spacing, level_index, plane_index,
     )
+    return received.astype(f32)
 
 
 def solution(mesh):

time: 69.8 us -> 58.2 us (0.83)
  Pallas kernels: 65.4 us -> 54.7 us
  local copies, waits for them, and re-layouts: 3.1 us -> 0 us
  other arithmetic: 0 us -> 2.77 us
    pallas_call x1, Pallas kernels: 65.4 us -> 54.7 us  [on_device(): pl.pallas_call(functools.partial(kernel, rows, groups), out_shape=jax.Sha...]
    unnamed x1 -> x0, local copies, waits for them, and re-layouts: 3.1 us -> none
    convert_element_type x0 -> x1, other arithmetic: none -> 2.77 us  [on_device(): return received.astype(f32)]
where the time goes in v2:
time: 58.2 us; the launch traced here: 57.5 us
  Pallas kernels  54.7 us (94%)
  other arithmetic  2.77 us (5%)
    pallas_call x1, Pallas kernels, on_device(): pl.pallas_call(functools.partial(kernel, rows, groups), out_shape=jax.Sha...  54.7 us
    convert_element_type x1, other arithmetic, on_device(): return received.astype(f32)  2.77 us

profile of v2, /device:TPU:0, one launch (start us, length us, event | category | flops | bytes accessed | tf_op | source)
XLA Modules:
  0.0 57.5 jit_solution(15998027863220544639)
XLA Ops:
  0.0 54.7 %shard_map.82 = bf16[2,8,128,256]{3,2,1,0:T(8,128)(2,1)} custom-call(bf16[2,8,128,256]{3,2,1,0:T(8,128)(2,1)} %vx.1, bf16[2,8,128,256]{3,2,1,0:T(8,128)(2,1)} %vy_hbm.1, bf16[2,8,128,256]{3,2,1,0:T(8,128)(2,1)} %vz_hbm.1, bf16[8,256,256]{2,1,0:T(8,128)(2,1)} %constant.4.clone.wh_hbm, bf16[8,256,256]{2,1,0:T(8,128)(2,1)} %constant.5.clone.wl_hbm, ...), custom_call_target="tpu_custom_call" | custom-call | tf_op jit(solution)/shard_map/pallas_call | solution.py:441
  54.7 2.8 %convert_element_type.3 = f32[2,8,128,256]{3,2,1,0:T(8,128)} convert(bf16[2,8,128,256]{3,2,1,0:T(8,128)(2,1)} %shard_map.82) | non-fusion elementwise | flops 524288 | bytes 3145728 | tf_op jit(solution)/shard_map/convert_element_type | solution.py:480

commit v3 on v2

--- a/solution.py
+++ b/solution.py
@@ -213,7 +213,7 @@
         return s * q, h_now, h_next, homog
 
     one = jnp.ones(tile, f32)
-    lax.fori_loop(0, depth, factor, (one, width_at(base - 1), width_at(base), one), unroll=4)
+    lax.fori_loop(0, depth, factor, (one, width_at(base - 1), width_at(base), one), unroll=8)
 
     def factor_back(t, carry):
         lo, hi = carry
@@ -226,7 +226,7 @@
         from_hi[rows_j, :] = hi
         return lo, hi
 
-    lax.fori_loop(0, depth, factor_back, (jnp.zeros(tile, f32), one), unroll=4)
+    lax.fori_loop(0, depth, factor_back, (jnp.zeros(tile, f32), one), unroll=16)
     top = (depth - 1) * RADIX
     coef[gz, 0] = from_lo[0:RADIX, :]
     coef[gz, 1] = from_hi[0:RADIX, :]
@@ -272,7 +272,7 @@
             combine(k, hat[:, :inner], hat[:, inner:])
             return carry
 
-        lax.fori_loop(0, RADIX, body, 0)
+        lax.fori_loop(0, RADIX, body, 0, unroll=4)
 
     def put_along(k, re, im):
         number = k + RADIX * lax.broadcasted_iota(jnp.int32, (1, inner), 1)
@@ -324,8 +324,8 @@
         return re, im
 
     zero = jnp.zeros(tile, f32)
-    lax.fori_loop(0, depth, sweep, (zero, zero), unroll=4)
-    lax.fori_loop(0, depth, sweep_back, (zero, zero), unroll=4)
+    lax.fori_loop(0, depth, sweep, (zero, zero), unroll=16)
+    lax.fori_loop(0, depth, sweep_back, (zero, zero), unroll=16)
 
     edge[gz, 0] = rhs_re[0:RADIX, :]
     edge[gz, 1] = rhs_re[top : top + RADIX, :]
@@ -382,7 +382,7 @@
     for z in range(depth // LANES):
         start = z * LANES
         cols = pl.ds(start, LANES)
-        lax.fori_loop(start, start + LANES, join, 0, unroll=4)
+        lax.fori_loop(start, start + LANES, join, 0, unroll=16)
 
         def inverse(k, carry):
             where = pl.ds(start * RADIX + k, LANES, stride=RADIX)
@@ -392,7 +392,7 @@
             spec[k] = dot(a, h, over_last) + dot(b, h, over_last) + dot(a, l, over_last)
             return carry
 
-        lax.fori_loop(0, RADIX, inverse, 0)
+        lax.fori_loop(0, RADIX, inverse, 0, unroll=4)
 
         def last_stage(t, carry):
             at = pl.multiple_of(t * step, step)

time: 58.2 us -> 55.8 us (0.959)
  Pallas kernels: 54.7 us -> 52.3 us
    pallas_call x1, Pallas kernels: 54.7 us -> 52.3 us  [on_device(): pl.pallas_call(functools.partial(kernel, rows, groups), out_shape=jax.Sha...]
where the time goes in v3:
time: 55.8 us; the launch traced here: 55.1 us
  Pallas kernels  52.3 us (94%)
  other arithmetic  2.77 us (5%)
    pallas_call x1, Pallas kernels, on_device(): pl.pallas_call(functools.partial(kernel, rows, groups), out_shape=jax.Sha...  52.3 us
    convert_element_type x1, other arithmetic, on_device(): return received.astype(f32)  2.77 us

profile of v3, /device:TPU:0, one launch (start us, length us, event | category | flops | bytes accessed | tf_op | source)
XLA Modules:
  0.0 55.1 jit_solution(3904260759681425775)
XLA Ops:
  0.0 52.3 %shard_map.82 = bf16[2,8,128,256]{3,2,1,0:T(8,128)(2,1)} custom-call(bf16[2,8,128,256]{3,2,1,0:T(8,128)(2,1)} %vx.1, bf16[2,8,128,256]{3,2,1,0:T(8,128)(2,1)} %vy_hbm.1, bf16[2,8,128,256]{3,2,1,0:T(8,128)(2,1)} %vz_hbm.1, bf16[8,256,256]{2,1,0:T(8,128)(2,1)} %constant.4.clone.wh_hbm, bf16[8,256,256]{2,1,0:T(8,128)(2,1)} %constant.5.clone.wl_hbm, ...), custom_call_target="tpu_custom_call" | custom-call | tf_op jit(solution)/shard_map/pallas_call | solution.py:441
  52.3 2.8 %convert_element_type.3 = f32[2,8,128,256]{3,2,1,0:T(8,128)} convert(bf16[2,8,128,256]{3,2,1,0:T(8,128)(2,1)} %shard_map.82) | non-fusion elementwise | flops 524288 | bytes 3145728 | tf_op jit(solution)/shard_map/convert_element_type | solution.py:480

commit v4 on v3

--- a/solution.py
+++ b/solution.py
@@ -169,15 +169,21 @@
         wave = jnp.full((1, depth), plane[p], jnp.int32).astype(f32) * wave_unit
         src[p, 0] = (-wave * vy[1, p].astype(f32) + slope_of(0, p)).astype(jnp.bfloat16)
         src[p, 1] = (wave * vy[0, p].astype(f32) + slope_of(1, p)).astype(jnp.bfloat16)
-
-        @pl.when(i > 0)
-        def _():
-            to_row(src.at[p], got_s.at[:, mine, :], s_send.at[i], s_recv.at[i], i).start()
-
         return carry
 
-    lax.fori_loop(1, rows, make_source, 0)
-    make_source(0, 0)
+    lax.fori_loop(0, rows, make_source, 0)
+    chunks = depth // LANES
+    sends_s = []
+    for z in range(chunks):
+        cols = pl.ds(z * LANES, LANES)
+        sends_s.append([])
+        for i in range(1, rows):
+            copy = to_row(
+                src.at[lax.rem(me + i, rows), :, :, cols], got_s.at[:, mine, cols],
+                s_send.at[z, i], s_recv.at[z, i], i,
+            )
+            copy.start()
+            sends_s[z].append(copy)
     own_s = pltpu.make_async_copy(src.at[me], got_s.at[:, mine, :], own_sem.at[1])
     own_s.start()
 
@@ -240,10 +246,10 @@
 
     step = 16
 
-    def first_stage(field):
+    def first_stage(field, begin, end):
         def body(t, carry):
             at = pl.multiple_of(t * step, step)
-            for lane in range(0, depth, LANES):
+            for lane in range(begin, end, LANES):
                 cols = pl.ds(lane, LANES)
                 re = [field[0, pl.ds(r * inner + at, step), cols].astype(f32) for r in range(RADIX)]
                 im = [field[1, pl.ds(r * inner + at, step), cols].astype(f32) for r in range(RADIX)]
@@ -257,7 +263,7 @@
                     yl[k, pl.ds(inner + at, step), cols] = l
             return carry
 
-        lax.fori_loop(0, inner // step, body, 0)
+        lax.fori_loop(0, inner // step, body, 0, unroll=2)
 
     over_rows = (((0,), (0,)), ((), ()))
     over_last = (((1,), (1,)), ((), ()))
@@ -265,43 +271,43 @@
     def dot(a, b, dims):
         return lax.dot_general(a, b, dims, preferred_element_type=f32)
 
-    def second_stage(combine):
+    def second_stage(combine, begin, end):
+        cols = pl.ds(begin, end - begin)
+
         def body(k, carry):
-            h, l, a, b = yh[k], yl[k], wh[k], wl[k]
+            h, l, a, b = yh[k, :, cols], yl[k, :, cols], wh[k], wl[k]
             hat = dot(h, a, over_rows) + dot(h, b, over_rows) + dot(l, a, over_rows)
-            combine(k, hat[:, :inner], hat[:, inner:])
+            where = pl.ds(begin * RADIX + k, end - begin, stride=RADIX)
+            combine(k, where, hat[:, :inner], hat[:, inner:])
             return carry
 
         lax.fori_loop(0, RADIX, body, 0, unroll=4)
 
-    def put_along(k, re, im):
+    def put_along(k, where, re, im):
         number = k + RADIX * lax.broadcasted_iota(jnp.int32, (1, inner), 1)
         column = jnp.where(number >= total_x // 2, number - total_x, number).astype(f32) * (
             full_turn / total_x
         )
-        where = pl.ds(k, depth, stride=RADIX)
         rhs_re[where, :] = -column * im
         rhs_im[where, :] = column * re
 
-    def put_source(k, re, im):
-        where = pl.ds(k, depth, stride=RADIX)
+    def put_source(k, where, re, im):
         rhs_re[where, :] = rhs_re[where, :] + re
         rhs_im[where, :] = rhs_im[where, :] + im
 
     own_u.wait()
     for copy in sends_u:
-        copy.wait()
+        copy.wait_recv()
     for load in loads[2:]:
         load.wait()
-    first_stage(got_u)
-    second_stage(put_along)
+    first_stage(got_u, 0, depth)
+    second_stage(put_along, 0, depth)
     own_s.wait()
-    for i in range(1, rows):
-        to_row(
-            src.at[lax.rem(me + i, rows)], got_s.at[:, mine, :], s_send.at[i], s_recv.at[i], i
-        ).wait()
-    first_stage(got_s)
-    second_stage(put_source)
+    for z in range(chunks):
+        for copy in sends_s[z]:
+            copy.wait_recv()
+        first_stage(got_s, z * LANES, (z + 1) * LANES)
+        second_stage(put_source, z * LANES, (z + 1) * LANES)
 
     def sweep(j, carry):
         re, im = carry
@@ -336,10 +342,8 @@
         copy = to_group(edge.at[gz], edge.at[gz], e_send.at[i], e_recv.at[i], i)
         copy.start()
         sends_e.append(copy)
-    for copy in sends_c:
-        copy.wait()
-    for copy in sends_e:
-        copy.wait()
+    for copy in sends_c + sends_e:
+        copy.wait_recv()
     if True:
         last_const, last_ratio = [(zero, zero)], [zero]
         head_const, head_ratio = [], []
@@ -418,6 +422,8 @@
         )
         copy.start()
         own_p.append(copy)
+    for copy in sends_u + sum(sends_s, []) + sends_c + sends_e:
+        copy.wait_send()
     for copy in own_p + sends_p:
         copy.wait()
 
@@ -465,7 +471,8 @@
             vmem((2, total_x, depth), bf16),
             dma((4,)),
             dma((2 + depth // LANES,)),
-            dma((rows,)), dma((rows,)), dma((rows,)), dma((rows,)),
+            dma((rows,)), dma((rows,)),
+            dma((depth // LANES, rows)), dma((depth // LANES, rows)),
             dma, dma,
             dma((groups,)), dma((groups,)), dma((groups,)), dma((groups,)),
             dma((depth // LANES, rows)), dma((depth // LANES, rows)),

time: 55.8 us -> 55.5 us (level)
  no operation moved by 1% of the time
where the time goes in v4:
time: 55.5 us; the launch traced here: 55.2 us
  Pallas kernels  52.4 us (94%)
  other arithmetic  2.77 us (5%)
    pallas_call x1, Pallas kernels, on_device(): pl.pallas_call(functools.partial(kernel, rows, groups), out_shape=jax.Sha...  52.4 us
    convert_element_type x1, other arithmetic, on_device(): return received.astype(f32)  2.77 us

profile of v4, /device:TPU:0, one launch (start us, length us, event | category | flops | bytes accessed | tf_op | source)
XLA Modules:
  0.0 55.2 jit_solution(17848357128146261779)
XLA Ops:
  0.0 52.4 %shard_map.82 = bf16[2,8,128,256]{3,2,1,0:T(8,128)(2,1)} custom-call(bf16[2,8,128,256]{3,2,1,0:T(8,128)(2,1)} %vx.1, bf16[2,8,128,256]{3,2,1,0:T(8,128)(2,1)} %vy_hbm.1, bf16[2,8,128,256]{3,2,1,0:T(8,128)(2,1)} %vz_hbm.1, bf16[8,256,256]{2,1,0:T(8,128)(2,1)} %constant.4.clone.wh_hbm, bf16[8,256,256]{2,1,0:T(8,128)(2,1)} %constant.5.clone.wl_hbm, ...), custom_call_target="tpu_custom_call" | custom-call | tf_op jit(solution)/shard_map/pallas_call | solution.py:447
  52.4 2.8 %convert_element_type.3 = f32[2,8,128,256]{3,2,1,0:T(8,128)} convert(bf16[2,8,128,256]{3,2,1,0:T(8,128)(2,1)} %shard_map.82) | non-fusion elementwise | flops 524288 | bytes 3145728 | tf_op jit(solution)/shard_map/convert_element_type | solution.py:487
